TPU v7x, 128 devices: a whole 4x4x4 slice. The times are simulated.
128 devices in a mesh: dp: 8 (over z, y_lo), tensor: 16 (over x, y_hi, core).
Axes of the slice: x: 4, y: 4 (y_hi: 2, y_lo: 2; y = y_hi * 2 + y_lo), z: 4, core: 2. Of those that a mesh axis runs over, the one named last changes fastest.
Arguments:
- projected: bfloat16 [2, 16384, 4608], P(None, ('dp', 'tensor')), may hold values from -60 to 60
- out_grad: bfloat16 [2, 16384, 4608], P(None, ('dp', 'tensor')), may hold values from -20 to 20
- attention: bfloat16 [2, 16384, 4096], P(None, 'dp', 'tensor'), may hold values from -6 to 6
- w_out: bfloat16 [4096, 4608], P('tensor'), may hold values from -0.09375 to 0.09375
- gains: float32 [4608], replicated, may hold values from 0.5 to 1.5
- main_out: float32 [4096, 4608], P('tensor', 'dp'), may hold values from -6 to 6
- main_gains: float32 [4608], replicated, may hold values from -6 to 6
Outputs:
- attn_grad: bfloat16 [2, 16384, 4096], P(None, 'dp', 'tensor')
- new_main_out: float32 [4096, 4608], P('tensor', 'dp')
- new_main_gains: float32 [4608], replicated
All inputs are finite; a program needn't handle non-finite values.
Results may differ from a plain program's by a relative error of at most 0.0049.
Values may be sent and summed in bfloat16 or wider, within the bound.
No kernel may reach another device: no remote copies, remote signals or barrier semaphores. Data moves between devices by JAX's collectives and lax.ppermute only.
A program may use at most 128 MiB of HBM per device.

v0:
```python
import functools
import math
import jax
import jax.numpy as jnp
from jax import lax
from jax.sharding import Mesh
from jax.sharding import PartitionSpec as P

DP = ("dp_0", "dp_1")
TENSOR = ("tensor_0", "tensor_1", "tensor_2")
DP_TENSOR = ("dp_0", "dp_1", "tensor_0", "tensor_1", "tensor_2")


def by_axis(value, axes):
    return functools.reduce(lax.psum, axes, value)


def cut_along(value, dim, size):
    before, after = (value.shape[:dim], value.shape[dim + 1 :])
    return jnp.moveaxis(value.reshape(*before, size, -1, *after), dim, 0)


def sent_and_summed(value, axis, dim):
    size = lax.axis_size(axis)
    parts = lax.all_to_all(cut_along(value, dim, size), axis, 0, 0, tiled=True)
    return jnp.sum(parts.astype(jnp.float32), axis=0)


def normalized(values):
    inverse = lax.rsqrt(jnp.mean(values * values, axis=-1, keepdims=True) + 1e-06)
    return (values * inverse, inverse)


def norm_back(upstream, normed, inverse):
    return inverse * (upstream - normed * jnp.mean(upstream * normed, axis=-1, keepdims=True))


def per_device(projected, out_grad, attention, w_out, gains, main_out, main_gains):
    micro_count = projected.shape[0]
    own_rows = projected.shape[1]
    tokens_all = micro_count * own_rows * lax.axis_size(DP) * lax.axis_size(TENSOR)
    factor = 1.0 / math.sqrt(tokens_all)
    gain_total = jnp.zeros(gains.shape, jnp.float32)
    back_list = []
    for micro_step in range(micro_count):
        output_in = projected[micro_step].astype(jnp.float32)
        upstream = out_grad[micro_step].astype(jnp.float32)
        out_hat, out_inv = normalized(output_in)
        out_gain = jnp.sum(upstream * out_hat, axis=0)
        out_back = norm_back(upstream * gains, out_hat, out_inv).astype(jnp.bfloat16)
        back_list.append(out_back)
        gain_total = gain_total + by_axis(out_gain, DP_TENSOR)
    stacked = jnp.stack(back_list)
    section = lax.all_gather(stacked, TENSOR, axis=1, tiled=True)
    weight_sum = lax.dot_general(
        attention, section, (((0, 1), (0, 1)), ((), ())), preferred_element_type=jnp.float32
    )
    product = lax.dot_general(
        section, w_out, (((2,), (1,)), ((), ())), preferred_element_type=jnp.float32
    ).astype(jnp.bfloat16)
    shard_out = sent_and_summed(weight_sum.astype(jnp.bfloat16), DP, 1)
    return (product, main_out + factor * shard_out, main_gains + factor * gain_total)


def solution(mesh):
    torus = Mesh(
        mesh.devices.reshape(4, 2, 4, 2, 2), ("dp_0", "dp_1", "tensor_0", "tensor_1", "tensor_2")
    )
    return jax.shard_map(
        per_device,
        mesh=torus,
        in_specs=(
            P(None, DP_TENSOR, None),
            P(None, DP_TENSOR, None),
            P(None, DP, TENSOR),
            P(TENSOR, None),
            P(),
            P(TENSOR, DP),
            P(),
        ),
        out_specs=(P(None, DP, TENSOR), P(TENSOR, DP), P()),
        check_vma=False,
    )
```

profile of v0, /device:TPU:1, one launch (start us, length us, event | category | flops | bytes accessed | tf_op | source)
XLA Modules:
  0.0 289.6 jit_solution(4183304599025154800)
XLA Ops:
  7.2 0.0 copy-start
  7.2 0.0 all-gather.2.cloned.1.call-start
  7.2 0.0 copy-start.1
  7.2 2.3 fusion.21
  9.6 0.2 copy-done.1
  9.8 3.5 %fusion.12 = (f32[128]{0:T(128)S(1)}, f32[128]{0:T(128)S(1)}, f32[4608]{0:T(1024)S(1)}, f32[4608]{0:T(1024)S(1)}) fusion(f32[128]{0:T(128)S(1)} %get-tuple-element.12, f32[4608]{0:T(1024)} %param.11, bf16[2,128,4608]{2,1,0:T(8,128)(2,1)} %param.8, bf16[2,128,4608]{2,1,0:T(8,128)(2,1)S(1)} %copy-done.1, f32[128]{0:T(128)S(1)} %get-tuple-element.11), kind=kLoop, calls=%fused_computation.23 | loop fusion | flops 9427712 | bytes 4775936 | tf_op jit(solution)/shard_map/reduce_sum | solution.py:35
  13.2 0.0 copy-done.2
  13.3 1.4 fusion.16
  14.7 1.6 pad_maximum_fusion
  16.3 0.0 all-gather.2.cloned.1.call-update
  16.3 15.3 %psum.84 = f32[4608]{0:T(1024)S(1)} all-reduce(f32[4608]{0:T(1024)S(1)} %add.48), channel_id=1, replica_groups=mesh['dp_0'=4,'dp_1'=2,'tensor_0'=4,'tensor_1'=2,'tensor_2'=2] {'dp_0'}, use_global_device_ids=true, to_apply=%region_6.0 | all-reduce | flops 4608 | bytes 36864 | tf_op jit(solution)/shard_map/psum | solution.py:15
  31.7 7.9 %psum.83 = f32[4608]{0:T(1024)S(1)} all-reduce(f32[4608]{0:T(1024)S(1)} %psum.84), channel_id=1, replica_groups=mesh['dp_0'=4,'dp_1'=2,'tensor_0'=4,'tensor_1'=2,'tensor_2'=2] {'dp_1'}, use_global_device_ids=true, to_apply=%region_7.0 | all-reduce | flops 4608 | bytes 36864 | tf_op jit(solution)/shard_map/psum | solution.py:15
  39.6 16.0 %psum.82 = f32[4608]{0:T(1024)S(1)} all-reduce(f32[4608]{0:T(1024)S(1)} %psum.83), channel_id=1, replica_groups=mesh['dp_0'=4,'dp_1'=2,'tensor_0'=4,'tensor_1'=2,'tensor_2'=2] {'tensor_0'}, use_global_device_ids=true, to_apply=%region_8.0 | all-reduce | flops 4608 | bytes 36864 | tf_op jit(solution)/shard_map/psum | solution.py:15
  55.5 9.5 %psum.81 = f32[4608]{0:T(1024)S(1)} all-reduce(f32[4608]{0:T(1024)S(1)} %psum.82), channel_id=1, replica_groups=mesh['dp_0'=4,'dp_1'=2,'tensor_0'=4,'tensor_1'=2,'tensor_2'=2] {'tensor_1'}, use_global_device_ids=true, to_apply=%region_9.0 | all-reduce | flops 4608 | bytes 36864 | tf_op jit(solution)/shard_map/psum | solution.py:15
  65.1 12.5 %psum.80 = f32[4608]{0:T(1024)S(1)} all-reduce(f32[4608]{0:T(1024)S(1)} %psum.81), channel_id=1, replica_groups=mesh['dp_0'=4,'dp_1'=2,'tensor_0'=4,'tensor_1'=2,'tensor_2'=2] {'tensor_2'}, use_global_device_ids=true, to_apply=%region_10.0 | all-reduce | flops 4608 | bytes 36864 | tf_op jit(solution)/shard_map/psum | solution.py:15
  77.5 0.6 multiply_add_fusion.1
  78.2 149.1 %all-gather.2.cloned.1.call-done = bf16[2,2048,4608]{2,1,0:T(8,128)(2,1)} async-done(((bf16[2,128,4608]{2,1,0:T(8,128)(2,1)}), bf16[2,2048,4608]{2,1,0:T(8,128)(2,1)}) %all-gather.2.cloned.1.call-update) | async-done | bytes 37748752 | tf_op jit(solution)/shard_map/all_gather | solution.py:54
  227.2 18.6 %fusion = bf16[4608,256]{1,0:T(8,128)(2,1)} fusion(bf16[2,2048,4608]{2,1,0:T(8,128)(2,1)} %all-gather.2.cloned.1.call-done, bf16[2,2048,256]{2,1,0:T(8,128)(2,1)} %param.9), kind=kOutput, calls=%fused_computation.1 | convolution fusion | flops 9664856064 | bytes 42205184 | tf_op jit(solution)/shard_map/dot_general | solution.py:55
  245.9 4.6 %all-to-all-start = ((bf16[8,256,576]{1,2,0:T(8,128)(2,1)}), bf16[8,256,576]{1,2,0:T(8,128)(2,1)}, u32[]{:S(2)}, u32[]{:S(2)}) async-start(bf16[8,256,576]{1,2,0:T(8,128)(2,1)} %bitcast.67), calls=%async_computation | async-start | bytes 4718592 | tf_op jit(solution)/shard_map/all_to_all | solution.py:25
  250.5 17.8 %convolution_convert_fusion = bf16[2,2048,256]{2,1,0:T(8,128)(2,1)} fusion(bf16[2,2048,4608]{2,1,0:T(8,128)(2,1)} %all-gather.2.cloned.1.call-done, bf16[256,4608]{1,0:T(8,128)(2,1)S(1)} %copy-done), kind=kOutput, calls=%fused_computation.3 | convolution fusion | flops 9664724992 | bytes 42205184 | tf_op jit(solution)/shard_map/dot_general | solution.py:58
  268.2 11.5 %all-to-all-done = bf16[8,256,576]{1,2,0:T(8,128)(2,1)} async-done(((bf16[8,256,576]{1,2,0:T(8,128)(2,1)}), bf16[8,256,576]{1,2,0:T(8,128)(2,1)}, u32[]{:S(2)}, u32[]{:S(2)}) %all-to-all-start) | async-done | bytes 2359328 | tf_op jit(solution)/shard_map/all_to_all | solution.py:25
  279.8 2.0 convert_reduce_fusion
  281.8 0.0 copy-done.3
  281.8 0.9 multiply_add_fusion
  (11 shorter events, 0.0 us)
Async XLA Ops:
  7.2 243.3 %copy-start = (bf16[256,4608]{1,0:T(8,128)(2,1)S(1)}, bf16[256,4608]{1,0:T(8,128)(2,1)}, u32[]{:S(2)}) copy-start(bf16[256,4608]{1,0:T(8,128)(2,1)} %param.10) | copy-start | bytes 7077892
  7.2 220.1 %all-gather.2.cloned.1.call-start = ((), (), s32[]{:S(2)}) async-start(), calls=%async_computation.1 | async-start | bytes 40108032 | tf_op jit(solution)/shard_map/all_gather | solution.py:54
  7.2 2.5 copy-start.1
  9.8 3.5 %copy-start.2 = (bf16[2,128,4608]{2,1,0:T(8,128)(2,1)S(1)}, bf16[2,128,4608]{2,1,0:T(8,128)(2,1)}, u32[]{:S(2)}) copy-start(bf16[2,128,4608]{2,1,0:T(8,128)(2,1)} %param.8) | copy-start | bytes 7077892
  9.8 3.5 %copy-start.4 = (f32[4608]{0:T(1024)S(1)}, f32[4608]{0:T(1024)}, u32[]{:S(2)}) copy-start(f32[4608]{0:T(1024)} %param.11) | copy-start | bytes 55300
  16.3 61.2 %copy-start.5 = (f32[4608]{0:T(1024)S(1)}, f32[4608]{0:T(1024)}, u32[]{:S(2)}) copy-start(f32[4608]{0:T(1024)} %param.13) | copy-start | bytes 55300
  245.9 33.9 %all-to-all-start = ((bf16[8,256,576]{1,2,0:T(8,128)(2,1)}), bf16[8,256,576]{1,2,0:T(8,128)(2,1)}, u32[]{:S(2)}, u32[]{:S(2)}) async-start(bf16[8,256,576]{1,2,0:T(8,128)(2,1)} %bitcast.67), calls=%async_computation | async-start | bytes 4718592 | tf_op jit(solution)/shard_map/all_to_all | solution.py:25
  268.2 13.6 %copy-start.3 = (f32[256,576]{0,1:T(8,128)S(1)}, f32[256,576]{0,1:T(8,128)}, u32[]{:S(2)}) copy-start(f32[256,576]{0,1:T(8,128)} %param.12) | copy-start | bytes 1769476
Sparse Core Ops, SparseCore 0:
  16.5 210.7 all-gather.1
where the time goes:
time: 290 us
  waiting for transfers between devices  161 us (56%)
  blocking collectives  61.2 us (21%)
  matrix products  36.4 us (13%)
  between operations  14.1 us (5%)
  other arithmetic  12.4 us (4%)
  starting transfers between devices  4.6 us (2%)
    all_gather x1, waiting for transfers between devices, per_device(): section = lax.all_gather(stacked, TENSOR, axis=1, tiled=True)  149 us
    psum x5, blocking collectives, by_axis(): return functools.reduce(lax.psum, axes, value)  61.2 us
    dot_general x1, matrix products, per_device(): lax.dot_general(attention, section, (((0, 1), (0, 1)), ((), ())), preferr...  18.6 us
    dot_general x1, matrix products, per_device(): lax.dot_general(section, w_out, (((2,), (1,)), ((), ())), preferred_eleme...  17.8 us
    all_to_all x1, waiting for transfers between devices, sent_and_summed(): parts = lax.all_to_all(cut_along(value, dim, size), axis, 0, 0, tiled=True)  11.5 us
  transfers between devices with their start and end apart: 2, of which 2 were waited for; matrix products, arithmetic and copies ran while one was open for 6% of the time, Pallas kernels for 0%

commit v1 on v0

--- a/solution.py
+++ b/solution.py
@@ -5,6 +5,7 @@
 from jax import lax
 from jax.sharding import Mesh
 from jax.sharding import PartitionSpec as P
+from jax.lax import all_to_all, axis_size
 
 DP = ("dp_0", "dp_1")
 TENSOR = ("tensor_0", "tensor_1", "tensor_2")
@@ -51,7 +52,9 @@
         back_list.append(out_back)
         gain_total = gain_total + by_axis(out_gain, DP_TENSOR)
     stacked = jnp.stack(back_list)
-    section = lax.all_gather(stacked, TENSOR, axis=1, tiled=True)
+    section = jnp.concatenate(
+        all_to_all(jnp.stack([stacked] * axis_size(TENSOR), 0), TENSOR, 0, 0), 1
+    )
     weight_sum = lax.dot_general(
         attention, section, (((0, 1), (0, 1)), ((), ())), preferred_element_type=jnp.float32
     )

time: 290 us -> 757 us (2.61)
  blocking collectives: 61.2 us -> 643 us
  waiting for transfers between devices: 161 us -> 11.8 us
  local copies, waits for them, and re-layouts: 0.2 us -> 38.7 us
  between operations: 14.1 us -> 0.73 us
  starting transfers between devices: 4.6 us -> 13.7 us
    psum x5, blocking collectives: 61.2 us -> 643 us  [by_axis(): return functools.reduce(lax.psum, axes, value)]
    all_gather x1 -> x0, waiting for transfers between devices: 149 us -> none  [per_device(): section = lax.all_gather(stacked, TENSOR, axis=1, tiled=True)]
    reshape x0 -> x1, local copies, waits for them, and re-layouts: none -> 25.8 us  [per_device(): jnp.concatenate(all_to_all(jnp.stack([stacked] * axis_size(TENSOR), 0), T...]
    another operation x0 -> x1, local copies, waits for them, and re-layouts: none -> 12.7 us  [per_device(): jnp.stack([stacked] * axis_size(TENSOR), 0)]
    all_to_all x0 -> x1, starting transfers between devices: none -> 8.57 us  [per_device(): all_to_all(jnp.stack([stacked] * axis_size(TENSOR), 0), TENSOR, 0, 0)]
  transfers between devices with their start and end apart: 2 -> 2, of which waited for: 2 -> 1; matrix products, arithmetic and copies ran while one was open for 6% -> 2% of each run, Pallas kernels for 0% -> 0%
where the time goes in v1:
time: 757 us; the launch traced here: 756 us
  blocking collectives  643 us (85%)
  local copies, waits for them, and re-layouts  38.7 us (5%)
  matrix products  36.4 us (5%)
  starting transfers between devices  13.7 us (2%)
  waiting for transfers between devices  11.8 us (2%)
  other arithmetic  11.1 us (1%)
    psum x5, blocking collectives, by_axis(): return functools.reduce(lax.psum, axes, value)  643 us
    reshape x1, local copies, waits for them, and re-layouts, per_device(): jnp.concatenate(all_to_all(jnp.stack([stacked] * axis_size(TENSOR), 0), T...  25.8 us
    dot_general x1, matrix products, per_device(): lax.dot_general(attention, section, (((0, 1), (0, 1)), ((), ())), preferr...  18.6 us
    dot_general x1, matrix products, per_device(): lax.dot_general(section, w_out, (((2,), (1,)), ((), ())), preferred_eleme...  17.7 us
  transfers between devices with their start and end apart: 2, of which 1 were waited for; matrix products, arithmetic and copies ran while one was open for 2% of the time, Pallas kernels for 0%

profile of v1, /device:TPU:1, one launch (start us, length us, event | category | flops | bytes accessed | tf_op | source)
XLA Modules:
  0.0 755.6 jit_solution(18152165219863923719)
XLA Ops:
  0.6 0.0 copy-start
  0.6 0.0 copy-start.1
  0.7 2.3 fusion.21
  3.0 0.2 copy-done.1
  3.2 3.5 fusion.12
  6.7 0.0 copy-done.2
  6.7 1.4 fusion.16
  8.1 0.2 pad_maximum_fusion
  8.3 12.7 %stack.5 = bf16[16,2,128,4608]{3,2,1,0:T(8,128)(2,1)} broadcast(bf16[2,128,4608]{2,1,0:T(8,128)(2,1)S(1)} %pad_maximum_fusion), dimensions={1,2,3} | broadcast | bytes 40108032 | tf_op jit(solution)/shard_map/stack | solution.py:56
  21.0 8.6 %all-to-all-start = ((bf16[16,2,128,4608]{3,2,1,0:T(8,128)(2,1)}), bf16[16,2,128,4608]{3,2,1,0:T(8,128)(2,1)}, u32[]{:S(2)}, u32[]{:S(2)}) async-start(bf16[16,2,128,4608]{3,2,1,0:T(8,128)(2,1)} %stack.5), calls=%async_computation | async-start | bytes 75497472 | tf_op jit(solution)/shard_map/all_to_all | solution.py:56
  29.6 16.1 %psum.84 = f32[4608]{0:T(1024)S(1)} all-reduce(f32[4608]{0:T(1024)S(1)} %add.48), channel_id=1, replica_groups=mesh['dp_0'=4,'dp_1'=2,'tensor_0'=4,'tensor_1'=2,'tensor_2'=2] {'dp_0'}, use_global_device_ids=true, to_apply=%region_6.0 | all-reduce | flops 4608 | bytes 36864 | tf_op jit(solution)/shard_map/psum | solution.py:16
  45.7 140.1 %psum.83 = f32[4608]{0:T(1024)S(1)} all-reduce(f32[4608]{0:T(1024)S(1)} %psum.84), channel_id=1, replica_groups=mesh['dp_0'=4,'dp_1'=2,'tensor_0'=4,'tensor_1'=2,'tensor_2'=2] {'dp_1'}, use_global_device_ids=true, to_apply=%region_7.0 | all-reduce | flops 4608 | bytes 36864 | tf_op jit(solution)/shard_map/psum | solution.py:16
  185.8 471.2 %psum.82 = f32[4608]{0:T(1024)S(1)} all-reduce(f32[4608]{0:T(1024)S(1)} %psum.83), channel_id=1, replica_groups=mesh['dp_0'=4,'dp_1'=2,'tensor_0'=4,'tensor_1'=2,'tensor_2'=2] {'tensor_0'}, use_global_device_ids=true, to_apply=%region_8.0 | all-reduce | flops 4608 | bytes 36864 | tf_op jit(solution)/shard_map/psum | solution.py:16
  657.1 6.6 psum.81
  663.7 9.2 %psum.80 = f32[4608]{0:T(1024)S(1)} all-reduce(f32[4608]{0:T(1024)S(1)} %psum.81), channel_id=1, replica_groups=mesh['dp_0'=4,'dp_1'=2,'tensor_0'=4,'tensor_1'=2,'tensor_2'=2] {'tensor_2'}, use_global_device_ids=true, to_apply=%region_10.0 | all-reduce | flops 4608 | bytes 36864 | tf_op jit(solution)/shard_map/psum | solution.py:16
  672.8 0.6 multiply_add_fusion.1
  673.4 0.0 all-to-all-done
  673.4 25.8 %copy.11 = bf16[2,16,128,4608]{3,2,1,0:T(8,128)(2,1)} copy(bf16[2,16,128,4608]{3,2,0,1:T(8,128)(2,1)} %bitcast.4) | data formatting | bytes 75497472 | tf_op jit(solution)/shard_map/reshape | solution.py:55
  699.3 18.6 %fusion = bf16[4608,256]{1,0:T(8,128)(2,1)} fusion(bf16[2,2048,4608]{2,1,0:T(8,128)(2,1)} %bitcast.69, bf16[2,2048,256]{2,1,0:T(8,128)(2,1)} %param.9), kind=kOutput, calls=%fused_computation.1 | convolution fusion | flops 9664856064 | bytes 42205184 | tf_op jit(solution)/shard_map/dot_general | solution.py:58
  717.9 5.1 all-to-all-start.1
  723.0 17.7 %convolution_convert_fusion = bf16[2,2048,256]{2,1,0:T(8,128)(2,1)} fusion(bf16[2,2048,4608]{2,1,0:T(8,128)(2,1)} %bitcast.70, bf16[256,4608]{1,0:T(8,128)(2,1)S(1)} %copy-done), kind=kOutput, calls=%fused_computation.3 | convolution fusion | flops 9664724992 | bytes 42205184 | tf_op jit(solution)/shard_map/dot_general | solution.py:61
  740.8 11.8 %all-to-all-done.1 = bf16[8,256,576]{1,2,0:T(8,128)(2,1)} async-done(((bf16[8,256,576]{1,2,0:T(8,128)(2,1)}), bf16[8,256,576]{1,2,0:T(8,128)(2,1)}, u32[]{:S(2)}, u32[]{:S(2)}) %all-to-all-start.1) | async-done | bytes 2359328 | tf_op jit(solution)/shard_map/all_to_all | solution.py:26
  752.6 2.0 convert_reduce_fusion
  754.6 0.9 multiply_add_fusion
  (12 shorter events, 0.0 us)
Async XLA Ops:
  0.6 722.4 %copy-start = (bf16[256,4608]{1,0:T(8,128)(2,1)S(1)}, bf16[256,4608]{1,0:T(8,128)(2,1)}, u32[]{:S(2)}) copy-start(bf16[256,4608]{1,0:T(8,128)(2,1)} %param.10) | copy-start | bytes 7077892
  0.6 2.5 copy-start.1
  3.2 3.5 copy-start.2
  3.2 3.5 copy-start.4
  21.0 651.8 %copy-start.5 = (f32[4608]{0:T(1024)S(1)}, f32[4608]{0:T(1024)}, u32[]{:S(2)}) copy-start(f32[4608]{0:T(1024)} %param.13) | copy-start | bytes 55300
  21.0 652.4 %all-to-all-start = ((bf16[16,2,128,4608]{3,2,1,0:T(8,128)(2,1)}), bf16[16,2,128,4608]{3,2,1,0:T(8,128)(2,1)}, u32[]{:S(2)}, u32[]{:S(2)}) async-start(bf16[16,2,128,4608]{3,2,1,0:T(8,128)(2,1)} %stack.5), calls=%async_computation | async-start | bytes 75497472 | tf_op jit(solution)/shard_map/all_to_all | solution.py:56
  717.9 34.7 %all-to-all-start.1 = ((bf16[8,256,576]{1,2,0:T(8,128)(2,1)}), bf16[8,256,576]{1,2,0:T(8,128)(2,1)}, u32[]{:S(2)}, u32[]{:S(2)}) async-start(bf16[8,256,576]{1,2,0:T(8,128)(2,1)} %bitcast.71), calls=%async_computation.1 | async-start | bytes 4718592 | tf_op jit(solution)/shard_map/all_to_all | solution.py:26
  740.8 13.8 %copy-start.3 = (f32[256,576]{0,1:T(8,128)S(1)}, f32[256,576]{0,1:T(8,128)}, u32[]{:S(2)}) copy-start(f32[256,576]{0,1:T(8,128)} %param.12) | copy-start | bytes 1769476
